TPU v7x, 32 devices: a whole 2x2x4 slice. The times are simulated.
32 devices in a mesh: paths: 4 (over x, core), cpty: 8 (over z, y).
Axes of the slice: x: 2, y: 2, z: 4, core: 2. Of those that a mesh axis runs over, the one named last changes fastest.
Arguments:
- factors: bfloat16 [64, 6144], P(None, 'paths'), may hold values from -6 to 6
- loadings: bfloat16 [64, 16384], P(None, 'cpty'), may hold values from -2 to 2
- notional: bfloat16 [16384], P('cpty'), may hold values from 0.25 to 0.796875
- strike: bfloat16 [16384], P('cpty'), may hold values from 2 to 8
- curvature: bfloat16 [16384], P('cpty'), may hold values from 1 to 3
- trade_cpty: int32 [16384], P('cpty'), may hold values from 0 to 1023, as said below
Outputs:
- exposure: bfloat16 [6144, 1024], P('paths', 'cpty')
- moment: float32 [1024, 1024], P('paths', 'cpty')
Inputs may be any that keep to these rules, and one draw needn't show every extreme that they name: `trade_cpty`: of the trades in the book of one index of cpty, at most 512 belong to the counterparties numbered k * 128 to (k + 1) * 128 - 1 for any k; in every draw some such k receives exactly 512 from every book.
All inputs are finite; a program needn't handle non-finite values.
Results may differ from a plain program's by a relative error of at most 0.0064.
Values may be sent and summed in bfloat16 or wider, within the bound.
No kernel may reach another device: no remote copies, remote signals or barrier semaphores. Data moves between devices by JAX's collectives and lax.ppermute only.
A program may use at most 128 MiB of HBM per device.

v0:
```python
import jax
import jax.numpy as jnp
from jax import lax
from jax.sharding import PartitionSpec as P

CP_DEV = 128


def price_trades(drivers, loading_cols, trade_terms):
    linear = jnp.dot(drivers, loading_cols, preferred_element_type=jnp.float32)
    terms_wide = trade_terms.astype(jnp.float32)
    value = terms_wide[0] * (linear + terms_wide[2] * jnp.tanh(linear - terms_wide[1]))
    return value.astype(jnp.bfloat16)


def on_device(factors, loadings, notional, strike, curvature, trade_cpty):
    groups = lax.axis_size("cpty")
    own_index = lax.axis_index("cpty")
    trades = loadings.shape[1]
    slot_size = 2 * trades // groups
    owners = trade_cpty // CP_DEV
    marked = (owners[:, None] == jnp.arange(groups, dtype=jnp.int32)[None, :]).astype(jnp.int32)
    ranking = jnp.sum((jnp.cumsum(marked, axis=0) - marked) * marked, axis=1)
    target = owners * slot_size + ranking
    chosen = (
        jnp.zeros((groups * slot_size,), jnp.int32)
        .at[target]
        .set(jnp.arange(trades, dtype=jnp.int32))
    )
    filled = jnp.zeros((groups * slot_size,), jnp.bool_).at[target].set(True)
    labels = jnp.where(filled, trade_cpty[chosen], -1)[None, :]
    drivers = jnp.transpose(factors)
    trade_terms = jnp.stack([notional, strike, curvature])
    described = jnp.concatenate([loadings, trade_terms], axis=0)
    packed = jnp.where(
        filled[None, :], jnp.take(described, chosen, axis=1), jnp.zeros((), jnp.bfloat16)
    )
    received, arrived_ids = (
        lax.all_to_all(packed, "cpty", split_axis=1, concat_axis=1, tiled=True),
        lax.all_to_all(labels, "cpty", split_axis=1, concat_axis=1, tiled=True),
    )
    factor_count = loadings.shape[0]
    arrived = price_trades(drivers, received[:factor_count], received[factor_count:])
    local_ids = arrived_ids[0] - own_index * CP_DEV
    onehot = (local_ids[:, None] == jnp.arange(CP_DEV, dtype=jnp.int32)[None, :]).astype(
        jnp.bfloat16
    )
    netted = jnp.dot(arrived, onehot, preferred_element_type=jnp.float32)
    exposure = jnp.maximum(netted, 0.0).astype(jnp.bfloat16)
    everyone = lax.all_gather(exposure, "cpty", axis=1, tiled=True)
    path_total = exposure.shape[0] * lax.axis_size("paths")
    moment = (
        lax.psum_scatter(
            jnp.einsum("pa,pb->ab", everyone, exposure, preferred_element_type=jnp.float32),
            "paths",
            scatter_dimension=0,
            tiled=True,
        )
        / path_total
    )
    return (exposure, moment)


def solution(mesh):
    in_specs = (P(None, "paths"), P(None, "cpty"), P("cpty"), P("cpty"), P("cpty"), P("cpty"))
    out_specs = (P("paths", "cpty"), P("paths", "cpty"))
    return jax.shard_map(
        on_device, mesh=mesh, in_specs=in_specs, out_specs=out_specs, check_vma=False
    )
```

profile of v0, /device:TPU:0, one launch (start us, length us, event | category | flops | bytes accessed | tf_op | source)
XLA Modules:
  0.0 204.9 jit_solution(14715116246756037690)
XLA Ops:
  7.2 0.8 add_select_fusion
  8.0 2.3 %reduce-window.6 = s32[8,16,128]{2,1,0:T(8,128)S(1)} reduce-window(s32[8,16,128]{2,1,0:T(8,128)S(1)} %fusion.14, s32[]{:T(128)} %constant.24.clone.1), window={size=1x1x128 pad=0_0x0_0x127_0}, to_apply=%region_0.1 | reduce-window | flops 2080768 | bytes 131076 | tf_op jit(solution)/shard_map/reduce-window
  10.3 0.3 slice_reduce_fusion
  10.9 0.7 compare_select_fusion.1
  11.6 8.1 %scatter_custom_fusion.1 = s32[4096]{0:T(1024)S(1)} fusion(s32[2048]{0:T(1024)S(1)} %compare_select_fusion.1, s32[2048]{0:T(1024)S(1)} %iota.15, s32[]{:T(128)} %constant.24.clone.1), kind=kCustom, calls=%fused_computation.43 | custom fusion | bytes 16388 | tf_op jit(solution)/shard_map/scatter | solution.py:28
  19.7 23.0 %gather_fusion.1 = s32[4096]{0:T(1024)S(1)} fusion(s32[2048]{0:T(1024)S(1)} %copy-done.1, s32[4096]{0:T(1024)S(1)} %fusion.15), kind=kCustom, calls=%fused_computation.1 | custom fusion | bytes 49152 | tf_op jit(solution)/shard_map/gather | solution.py:31
  42.8 9.1 %scatter_custom_fusion = pred[4096]{0:T(1024)(128)(4,1)S(1)} fusion(s32[2048]{0:T(1024)S(1)} %compare_select_fusion.1, pred[2048]{0:T(1024)(128)(4,1)S(1)} %broadcast.49, pred[]{:T(512)} %constant.22.clone.1), kind=kCustom, calls=%fused_computation.47 | custom fusion | bytes 4097 | tf_op jit(solution)/shard_map/scatter | solution.py:30
  51.9 0.6 broadcast_select_fusion
  52.5 7.3 %all-to-all-start.1 = ((s32[1,8,512]{2,0,1:T(1,128)}), s32[1,8,512]{2,0,1:T(1,128)S(1)}, u32[]{:S(2)}, u32[]{:S(2)}) async-start(s32[1,8,512]{2,0,1:T(1,128)} %bitcast.8), calls=%async_computation.1 | async-start | bytes 32768 | tf_op jit(solution)/shard_map/all_to_all | solution.py:40
  60.2 0.3 stack.12
  60.5 0.3 stack.13
  60.9 0.3 stack.14
  61.2 0.7 pad_maximum_fusion
  61.9 12.1 %gather_fusion = bf16[4096,67]{1,0:T(8,128)(2,1)S(1)} fusion(bf16[67,2048]{0,1:T(8,128)(2,1)S(1)} %pad_maximum_fusion, s32[4096]{0:T(1024)S(1)} %fusion.15), kind=kCustom, calls=%fused_computation | custom fusion | bytes 1114112 | tf_op jit(solution)/shard_map/jit(_take)/gather | solution.py:36
  74.1 0.6 copy.23
  74.6 0.9 select_select_fusion
  75.5 6.0 %all-to-all-start = ((bf16[67,8,512]{2,0,1:T(8,128)(2,1)}), bf16[67,8,512]{2,0,1:T(8,128)(2,1)S(1)}, u32[]{:S(2)}, u32[]{:S(2)}) async-start(bf16[67,8,512]{2,0,1:T(8,128)(2,1)} %select_select_fusion), calls=%async_computation | async-start | bytes 1179648 | tf_op jit(solution)/shard_map/all_to_all | solution.py:39
  81.6 0.9 iota_compare_fusion.7
  82.5 14.4 %all-to-all-done = bf16[67,8,512]{2,0,1:T(8,128)(2,1)S(1)} async-done(((bf16[67,8,512]{2,0,1:T(8,128)(2,1)}), bf16[67,8,512]{2,0,1:T(8,128)(2,1)S(1)}, u32[]{:S(2)}, u32[]{:S(2)}) %all-to-all-start) | async-done | bytes 548896 | tf_op jit(solution)/shard_map/all_to_all | solution.py:39
  97.1 13.8 %fusion.9 = bf16[1536,128]{1,0:T(8,128)(2,1)} fusion(bf16[64,4096]{1,0:T(8,128)(2,1)S(1)} %bitcast.70, bf16[64,1536]{1,0:T(8,128)(2,1)S(1)} %copy-done, f32[4096]{0:T(1024)S(1)} %bitcast.75, f32[4096]{0:T(1024)S(1)} %bitcast.76, f32[4096]{0:T(1024)S(1)} %bitcast.74, pred[4096,128]{1,0:T(32,128)(4,1)S(1)} %iota_compare_fusion.7), kind=kOutput, calls=%fused_computation.15 | convolution fusion | flops 2447769600 | bytes 1687552 | tf_op jit(solution)/shard_map/dot_general | solution.py:48
  110.9 61.8 %all-gather.2.cloned.1.call-done = bf16[1536,1024]{1,0:T(8,128)(2,1)} async-done(((bf16[1536,128]{1,0:T(8,128)(2,1)}), bf16[1536,1024]{1,0:T(8,128)(2,1)}) %all-gather.2.cloned.1.call-update) | async-done | bytes 3145744 | tf_op jit(solution)/shard_map/all_gather | solution.py:50
  172.7 3.7 %fusion.24 = f32[1024,128]{1,0:T(8,128)} fusion(bf16[1536,1024]{1,0:T(8,128)(2,1)} %all-gather.2.cloned.1.call-done, bf16[1536,128]{1,0:T(8,128)(2,1)} %fusion.9), kind=kOutput, calls=%fused_computation.51 | convolution fusion | flops 402653184 | bytes 4063232 | tf_op jit(solution)/shard_map/pa,pb->ab/dot_general | solution.py:54
  176.5 20.0 %reduce-scatter.2.cloned.1.call-done = f32[256,128]{1,0:T(8,128)} async-done(((f32[1024,128]{1,0:T(8,128)}), f32[256,128]{1,0:T(8,128)}) %reduce-scatter.2.cloned.1.call-update) | async-done | bytes 131088 | tf_op jit(solution)/shard_map/reduce_scatter | solution.py:53
  196.4 1.6 broadcast_multiply_fusion
  (33 shorter events, 0.9 us)
Async XLA Ops:
  7.2 89.9 %copy-start = (bf16[64,1536]{1,0:T(8,128)(2,1)S(1)}, bf16[64,1536]{1,0:T(8,128)(2,1)}, u32[]{:S(2)}) copy-start(bf16[64,1536]{1,0:T(8,128)(2,1)} %param.6) | copy-start | bytes 589828
  7.2 12.5 %copy-start.1 = (s32[2048]{0:T(1024)S(1)}, s32[2048]{0:T(1024)}, u32[]{:S(2)}) copy-start(s32[2048]{0:T(1024)} %param.11) | copy-start | bytes 24580
  19.7 40.2 %copy-start.2 = (bf16[64,2048]{1,0:T(8,128)(2,1)S(1)}, bf16[64,2048]{1,0:T(8,128)(2,1)}, u32[]{:S(2)}) copy-start(bf16[64,2048]{1,0:T(8,128)(2,1)} %param.7) | copy-start | bytes 786436
  19.7 40.5 %copy-start.3 = (bf16[2048]{0:T(1024)(128)(2,1)S(1)}, bf16[2048]{0:T(1024)(128)(2,1)}, u32[]{:S(2)}) copy-start(bf16[2048]{0:T(1024)(128)(2,1)} %param.8) | copy-start | bytes 12292
  19.7 40.8 %copy-start.4 = (bf16[2048]{0:T(1024)(128)(2,1)S(1)}, bf16[2048]{0:T(1024)(128)(2,1)}, u32[]{:S(2)}) copy-start(bf16[2048]{0:T(1024)(128)(2,1)} %param.9) | copy-start | bytes 12292
  19.7 41.2 %copy-start.5 = (bf16[2048]{0:T(1024)(128)(2,1)S(1)}, bf16[2048]{0:T(1024)(128)(2,1)}, u32[]{:S(2)}) copy-start(bf16[2048]{0:T(1024)(128)(2,1)} %param.10) | copy-start | bytes 12292
  52.5 23.0 %all-to-all-start.1 = ((s32[1,8,512]{2,0,1:T(1,128)}), s32[1,8,512]{2,0,1:T(1,128)S(1)}, u32[]{:S(2)}, u32[]{:S(2)}) async-start(s32[1,8,512]{2,0,1:T(1,128)} %bitcast.8), calls=%async_computation.1 | async-start | bytes 32768 | tf_op jit(solution)/shard_map/all_to_all | solution.py:40
  75.5 21.4 %all-to-all-start = ((bf16[67,8,512]{2,0,1:T(8,128)(2,1)}), bf16[67,8,512]{2,0,1:T(8,128)(2,1)S(1)}, u32[]{:S(2)}, u32[]{:S(2)}) async-start(bf16[67,8,512]{2,0,1:T(8,128)(2,1)} %select_select_fusion), calls=%async_computation | async-start | bytes 1179648 | tf_op jit(solution)/shard_map/all_to_all | solution.py:39
  81.5 91.2 %all-gather.2.cloned.1.call-start = ((), (), s32[]{:S(2)}) async-start(), calls=%async_computation.3 | async-start | bytes 3538944 | tf_op jit(solution)/shard_map/all_gather | solution.py:50
  110.9 85.6 %reduce-scatter.2.cloned.1.call-start = ((), (), s32[]{:S(2)}) async-start(), calls=%async_computation.4 | async-start | bytes 655360 | tf_op jit(solution)/shard_map/reduce_scatter | solution.py:53
Sparse Core Ops, SparseCore 0:
  111.0 61.6 all-gather.1
  176.6 19.7 reduce-scatter.1
where the time goes:
time: 205 us
  waiting for transfers between devices  96.2 us (47%)
  local copies, waits for them, and re-layouts  54.7 us (27%)
  matrix products  17.5 us (9%)
  between operations  14.3 us (7%)
  starting transfers between devices  13.4 us (7%)
  other arithmetic  8.76 us (4%)
    all_gather x1, waiting for transfers between devices, on_device(): everyone = lax.all_gather(exposure, 'cpty', axis=1, tiled=True)  61.8 us
    gather x1, local copies, waits for them, and re-layouts, on_device(): labels = jnp.where(filled, trade_cpty[chosen], -1)[None, :]  23 us
    reduce_scatter x1, waiting for transfers between devices, on_device(): lax.psum_scatter(jnp.einsum('pa,pb->ab', everyone, exposure, preferred_el...  20 us
    all_to_all x1, waiting for transfers between devices, on_device(): lax.all_to_all(packed, 'cpty', split_axis=1, concat_axis=1, tiled=True)  14.4 us
    dot_general x1, matrix products, on_device(): netted = jnp.dot(arrived, onehot, preferred_element_type=jnp.float32)  13.8 us
    gather x2, local copies, waits for them, and re-layouts, on_device(): jnp.take(described, chosen, axis=1)  12.7 us
    scatter x1, local copies, waits for them, and re-layouts, on_device(): filled = jnp.zeros((groups * slot_size,), jnp.bool_).at[target].set(True)  9.13 us
    scatter x1, local copies, waits for them, and re-layouts, on_device(): chosen = jnp.zeros((groups * slot_size,), jnp.int32).at[target].set(jnp.a...  8.06 us
  transfers between devices with their start and end apart: 4, of which 3 were waited for; matrix products, arithmetic and copies ran while one was open for 8% of the time, Pallas kernels for 0%

commit v1 on v0

--- a/solution.py
+++ b/solution.py
@@ -47,7 +47,7 @@
     )
     netted = jnp.dot(arrived, onehot, preferred_element_type=jnp.float32)
     exposure = jnp.maximum(netted, 0.0).astype(jnp.bfloat16)
-    everyone = lax.all_gather(exposure, "cpty", axis=1, tiled=True)
+    everyone = jnp.concatenate(lax.all_gather(exposure, "cpty"), axis=1)
     path_total = exposure.shape[0] * lax.axis_size("paths")
     moment = (
         lax.psum_scatter(

time: 205 us -> 205 us (level)
  local copies, waits for them, and re-layouts: 54.7 us -> 57.9 us
  waiting for transfers between devices: 96.2 us -> 94.1 us
    all_gather x0 -> x1, local copies, waits for them, and re-layouts: none -> 3.18 us  [on_device(): everyone = jnp.concatenate(lax.all_gather(exposure, 'cpty'), axis=1)]
    all_gather x1, waiting for transfers between devices: 61.8 us -> 59.2 us  [on_device(): everyone = jnp.concatenate(lax.all_gather(exposure, 'cpty'), axis=1)]
where the time goes in v1:
time: 205 us
  waiting for transfers between devices  94.1 us (46%)
  local copies, waits for them, and re-layouts  57.9 us (28%)
  matrix products  16.5 us (8%)
  between operations  14.3 us (7%)
  starting transfers between devices  13.4 us (7%)
  other arithmetic  8.76 us (4%)
    all_gather x1, waiting for transfers between devices, on_device(): everyone = jnp.concatenate(lax.all_gather(exposure, 'cpty'), axis=1)  59.2 us
    gather x1, local copies, waits for them, and re-layouts, on_device(): labels = jnp.where(filled, trade_cpty[chosen], -1)[None, :]  23 us
    reduce_scatter x1, waiting for transfers between devices, on_device(): lax.psum_scatter(jnp.einsum('pa,pb->ab', everyone, exposure, preferred_el...  20.5 us
    all_to_all x1, waiting for transfers between devices, on_device(): lax.all_to_all(packed, 'cpty', split_axis=1, concat_axis=1, tiled=True)  14.4 us
    dot_general x1, matrix products, on_device(): netted = jnp.dot(arrived, onehot, preferred_element_type=jnp.float32)  13.8 us
    gather x2, local copies, waits for them, and re-layouts, on_device(): jnp.take(described, chosen, axis=1)  12.7 us
    scatter x1, local copies, waits for them, and re-layouts, on_device(): filled = jnp.zeros((groups * slot_size,), jnp.bool_).at[target].set(True)  9.13 us
    scatter x1, local copies, waits for them, and re-layouts, on_device(): chosen = jnp.zeros((groups * slot_size,), jnp.int32).at[target].set(jnp.a...  8.06 us
  transfers between devices with their start and end apart: 4, of which 3 were waited for; matrix products, arithmetic and copies ran while one was open for 8% of the time, Pallas kernels for 0%

profile of v1, /device:TPU:0, one launch (start us, length us, event | category | flops | bytes accessed | tf_op | source)
XLA Modules:
  0.0 205.0 jit_solution(950302255255442821)
XLA Ops:
  7.2 0.8 add_select_fusion
  8.0 2.3 %reduce-window.6 = s32[8,16,128]{2,1,0:T(8,128)S(1)} reduce-window(s32[8,16,128]{2,1,0:T(8,128)S(1)} %fusion.14, s32[]{:T(128)} %constant.24.clone.1), window={size=1x1x128 pad=0_0x0_0x127_0}, to_apply=%region_0.1 | reduce-window | flops 2080768 | bytes 131076 | tf_op jit(solution)/shard_map/reduce-window
  10.9 0.7 compare_select_fusion.1
  11.6 8.1 %scatter_custom_fusion.1 = s32[4096]{0:T(1024)S(1)} fusion(s32[2048]{0:T(1024)S(1)} %compare_select_fusion.1, s32[2048]{0:T(1024)S(1)} %iota.15, s32[]{:T(128)} %constant.24.clone.1), kind=kCustom, calls=%fused_computation.43 | custom fusion | bytes 16388 | tf_op jit(solution)/shard_map/scatter | solution.py:28
  19.7 23.0 %gather_fusion.1 = s32[4096]{0:T(1024)S(1)} fusion(s32[2048]{0:T(1024)S(1)} %copy-done.1, s32[4096]{0:T(1024)S(1)} %fusion.15), kind=kCustom, calls=%fused_computation.1 | custom fusion | bytes 49152 | tf_op jit(solution)/shard_map/gather | solution.py:31
  42.8 9.1 %scatter_custom_fusion = pred[4096]{0:T(1024)(128)(4,1)S(1)} fusion(s32[2048]{0:T(1024)S(1)} %compare_select_fusion.1, pred[2048]{0:T(1024)(128)(4,1)S(1)} %broadcast.49, pred[]{:T(512)} %constant.22.clone.1), kind=kCustom, calls=%fused_computation.47 | custom fusion | bytes 4097 | tf_op jit(solution)/shard_map/scatter | solution.py:30
  51.9 0.6 broadcast_select_fusion
  52.5 7.3 %all-to-all-start.1 = ((s32[1,8,512]{2,0,1:T(1,128)}), s32[1,8,512]{2,0,1:T(1,128)S(1)}, u32[]{:S(2)}, u32[]{:S(2)}) async-start(s32[1,8,512]{2,0,1:T(1,128)} %bitcast.8), calls=%async_computation.1 | async-start | bytes 32768 | tf_op jit(solution)/shard_map/all_to_all | solution.py:40
  60.2 0.3 stack.12
  60.5 0.3 stack.13
  60.9 0.3 stack.14
  61.2 0.7 pad_maximum_fusion
  61.9 12.1 %gather_fusion = bf16[4096,67]{1,0:T(8,128)(2,1)S(1)} fusion(bf16[67,2048]{0,1:T(8,128)(2,1)S(1)} %pad_maximum_fusion, s32[4096]{0:T(1024)S(1)} %fusion.15), kind=kCustom, calls=%fused_computation | custom fusion | bytes 1114112 | tf_op jit(solution)/shard_map/jit(_take)/gather | solution.py:36
  74.1 0.6 copy.25
  74.6 0.9 select_select_fusion
  75.5 6.0 %all-to-all-start = ((bf16[67,8,512]{2,0,1:T(8,128)(2,1)}), bf16[67,8,512]{2,0,1:T(8,128)(2,1)S(1)}, u32[]{:S(2)}, u32[]{:S(2)}) async-start(bf16[67,8,512]{2,0,1:T(8,128)(2,1)} %select_select_fusion), calls=%async_computation | async-start | bytes 1179648 | tf_op jit(solution)/shard_map/all_to_all | solution.py:39
  81.6 0.9 iota_compare_fusion.7
  82.5 14.4 %all-to-all-done = bf16[67,8,512]{2,0,1:T(8,128)(2,1)S(1)} async-done(((bf16[67,8,512]{2,0,1:T(8,128)(2,1)}), bf16[67,8,512]{2,0,1:T(8,128)(2,1)S(1)}, u32[]{:S(2)}, u32[]{:S(2)}) %all-to-all-start) | async-done | bytes 548896 | tf_op jit(solution)/shard_map/all_to_all | solution.py:39
  97.1 13.8 %fusion.9 = bf16[1536,128]{1,0:T(8,128)(2,1)} fusion(bf16[64,4096]{1,0:T(8,128)(2,1)S(1)} %bitcast.76, bf16[64,1536]{1,0:T(8,128)(2,1)S(1)} %copy-done, f32[4096]{0:T(1024)S(1)} %bitcast.81, f32[4096]{0:T(1024)S(1)} %bitcast.82, f32[4096]{0:T(1024)S(1)} %bitcast.80, pred[4096,128]{1,0:T(32,128)(4,1)S(1)} %iota_compare_fusion.7), kind=kOutput, calls=%fused_computation.15 | convolution fusion | flops 2447769600 | bytes 1687552 | tf_op jit(solution)/shard_map/dot_general | solution.py:48
  110.9 59.2 %all-gather.3.cloned.1.call-done = bf16[12288,128]{1,0:T(8,128)(2,1)} async-done(((bf16[1536,128]{1,0:T(8,128)(2,1)}), bf16[12288,128]{1,0:T(8,128)(2,1)}) %all-gather.3.cloned.1.call-update) | async-done | bytes 3145744 | tf_op jit(solution)/shard_map/all_gather | solution.py:50
  170.1 3.2 %copy.27 = bf16[8,1536,128]{1,2,0:T(8,128)(2,1)S(1)} copy(bf16[8,1536,128]{2,1,0:T(8,128)(2,1)} %bitcast.74) | data formatting | bytes 6291456 | tf_op jit(solution)/shard_map/all_gather | solution.py:50
  173.3 2.8 %fusion.24 = f32[1024,128]{1,0:T(8,128)} fusion(bf16[1536,1024]{0,1:T(8,128)(2,1)S(1)} %bitcast.73, bf16[1536,128]{1,0:T(8,128)(2,1)} %fusion.9), kind=kOutput, calls=%fused_computation.51 | convolution fusion | flops 402653184 | bytes 4063232 | tf_op jit(solution)/shard_map/pa,pb->ab/dot_general | solution.py:54
  176.1 20.5 %reduce-scatter.2.cloned.1.call-done = f32[256,128]{1,0:T(8,128)} async-done(((f32[1024,128]{1,0:T(8,128)}), f32[256,128]{1,0:T(8,128)}) %reduce-scatter.2.cloned.1.call-update) | async-done | bytes 131088 | tf_op jit(solution)/shard_map/reduce_scatter | solution.py:53
  196.6 1.6 broadcast_multiply_fusion
  (34 shorter events, 1.2 us)
Async XLA Ops:
  7.2 89.9 %copy-start = (bf16[64,1536]{1,0:T(8,128)(2,1)S(1)}, bf16[64,1536]{1,0:T(8,128)(2,1)}, u32[]{:S(2)}) copy-start(bf16[64,1536]{1,0:T(8,128)(2,1)} %param.6) | copy-start | bytes 589828
  7.2 12.5 %copy-start.1 = (s32[2048]{0:T(1024)S(1)}, s32[2048]{0:T(1024)}, u32[]{:S(2)}) copy-start(s32[2048]{0:T(1024)} %param.11) | copy-start | bytes 24580
  19.7 40.2 %copy-start.2 = (bf16[64,2048]{1,0:T(8,128)(2,1)S(1)}, bf16[64,2048]{1,0:T(8,128)(2,1)}, u32[]{:S(2)}) copy-start(bf16[64,2048]{1,0:T(8,128)(2,1)} %param.7) | copy-start | bytes 786436
  19.7 40.5 %copy-start.3 = (bf16[2048]{0:T(1024)(128)(2,1)S(1)}, bf16[2048]{0:T(1024)(128)(2,1)}, u32[]{:S(2)}) copy-start(bf16[2048]{0:T(1024)(128)(2,1)} %param.8) | copy-start | bytes 12292
  19.7 40.8 %copy-start.4 = (bf16[2048]{0:T(1024)(128)(2,1)S(1)}, bf16[2048]{0:T(1024)(128)(2,1)}, u32[]{:S(2)}) copy-start(bf16[2048]{0:T(1024)(128)(2,1)} %param.9) | copy-start | bytes 12292
  19.7 41.2 %copy-start.5 = (bf16[2048]{0:T(1024)(128)(2,1)S(1)}, bf16[2048]{0:T(1024)(128)(2,1)}, u32[]{:S(2)}) copy-start(bf16[2048]{0:T(1024)(128)(2,1)} %param.10) | copy-start | bytes 12292
  52.5 23.0 %all-to-all-start.1 = ((s32[1,8,512]{2,0,1:T(1,128)}), s32[1,8,512]{2,0,1:T(1,128)S(1)}, u32[]{:S(2)}, u32[]{:S(2)}) async-start(s32[1,8,512]{2,0,1:T(1,128)} %bitcast.8), calls=%async_computation.1 | async-start | bytes 32768 | tf_op jit(solution)/shard_map/all_to_all | solution.py:40
  75.5 21.4 %all-to-all-start = ((bf16[67,8,512]{2,0,1:T(8,128)(2,1)}), bf16[67,8,512]{2,0,1:T(8,128)(2,1)S(1)}, u32[]{:S(2)}, u32[]{:S(2)}) async-start(bf16[67,8,512]{2,0,1:T(8,128)(2,1)} %select_select_fusion), calls=%async_computation | async-start | bytes 1179648 | tf_op jit(solution)/shard_map/all_to_all | solution.py:39
  81.5 88.5 %all-gather.3.cloned.1.call-start = ((), (), s32[]{:S(2)}) async-start(), calls=%async_computation.4 | async-start | bytes 3538944 | tf_op jit(solution)/shard_map/all_gather | solution.py:50
  110.9 85.7 %reduce-scatter.2.cloned.1.call-start = ((), (), s32[]{:S(2)}) async-start(), calls=%async_computation.3 | async-start | bytes 655360 | tf_op jit(solution)/shard_map/reduce_scatter | solution.py:53
Sparse Core Ops, SparseCore 0:
  111.0 59.0 all-gather.2
  176.2 20.3 reduce-scatter.1
